TPU v7x, 32 devices: a whole 2x2x4 slice. The times are simulated.
32 devices in a mesh: dp: 8 (over z, y), tensor: 4 (over x, core).
Axes of the slice: x: 2, y: 2, z: 4, core: 2. Of those that a mesh axis runs over, the one named last changes fastest.
Arguments:
- tokens: bfloat16 [16384, 768], P(('dp', 'tensor')), may hold values from -6 to 6
- seq_lengths: int32 [16], P('dp'), may hold values from 100 to 1024, as said below
- cotangent: bfloat16 [16384, 768], P(('dp', 'tensor')), may hold values from -6 to 6
- ln1_gain: bfloat16 [768], replicated, may hold values from 0.5 to 1.5
- ln1_shift: bfloat16 [768], replicated, may hold values from -2 to 2
- w_qkv: bfloat16 [768, 3, 768], P(None, None, 'tensor'), may hold values from -0.21875 to 0.21875
- b_qkv: bfloat16 [3, 768], P(None, 'tensor'), may hold values from -2 to 2
- w_out: bfloat16 [768, 768], P('tensor'), may hold values from -1.25 to 1.25
- b_out: bfloat16 [768], replicated, may hold values from -2 to 2
- ln2_gain: bfloat16 [768], replicated, may hold values from 0.5 to 1.5
- ln2_shift: bfloat16 [768], replicated, may hold values from -2 to 2
- w_up: bfloat16 [768, 3072], P(None, 'tensor'), may hold values from -0.21875 to 0.21875
- b_up: bfloat16 [3072], P('tensor'), may hold values from -2 to 2
- w_down: bfloat16 [3072, 768], P('tensor'), may hold values from -0.109375 to 0.109375
- b_down: bfloat16 [768], replicated, may hold values from -2 to 2
Outputs:
- output: bfloat16 [16384, 768], P(('dp', 'tensor'))
- grad_tokens: bfloat16 [16384, 768], P(('dp', 'tensor'))
- grad_ln1_gain: float32 [768], replicated
- grad_ln1_shift: float32 [768], replicated
- grad_w_qkv: float32 [768, 3, 768], P(None, None, 'tensor')
- grad_b_qkv: float32 [3, 768], P(None, 'tensor')
- grad_w_out: float32 [768, 768], P('tensor')
- grad_b_out: float32 [768], replicated
- grad_ln2_gain: float32 [768], replicated
- grad_ln2_shift: float32 [768], replicated
- grad_w_up: float32 [768, 3072], P(None, 'tensor')
- grad_b_up: float32 [3072], P('tensor')
- grad_w_down: float32 [3072, 768], P('tensor')
- grad_b_down: float32 [768], replicated
Inputs may be any that keep to these rules, and one draw needn't show every extreme that they name: `seq_lengths`: number of codons of each sequence; one sequence has exactly 1024 and one exactly 100; short sequences are more common than long ones.
All inputs are finite; a program needn't handle non-finite values.
Results may differ from a plain program's by a relative error of at most 0.013.
Values may be sent and summed in bfloat16 or wider, within the bound.
A program may use at most 128 MiB of HBM per device.

v0:
```python
import math
import jax
import jax.numpy as jnp
from jax import lax
from jax.sharding import PartitionSpec as P

HEAD_DIM = 64
SEQ = 1024
norm_eps = 1e-05
mask_fill = -1e30


def layer_norm(values, ln_gain, ln_shift):
    row_mean = jnp.mean(values, axis=-1, keepdims=True)
    centred = values - row_mean
    row_var = jnp.mean(centred * centred, axis=-1, keepdims=True)
    return centred * lax.rsqrt(row_var + norm_eps) * ln_gain + ln_shift


def rotary_tables():
    half_dim = HEAD_DIM // 2
    inverse_freq = jnp.exp(
        jnp.arange(half_dim, dtype=jnp.float32) * (-2.0 * math.log(10000.0) / HEAD_DIM)
    )
    angles = jnp.arange(SEQ, dtype=jnp.float32)[:, None] * inverse_freq[None, :]
    return (jnp.cos(angles), jnp.sin(angles))


def rotate(head_vals, cosine, sine_table):
    half_dim = head_vals.shape[-1] // 2
    lower_half = head_vals[..., :half_dim]
    upper_half = head_vals[..., half_dim:]
    cos_part = cosine[:, None, :]
    sin_part = sine_table[:, None, :]
    return jnp.concatenate(
        [
            lower_half * cos_part - upper_half * sin_part,
            upper_half * cos_part + lower_half * sin_part,
        ],
        axis=-1,
    )


def contract_last(left_mat, right_mat):
    return lax.dot_general(
        left_mat, right_mat, (((1,), (1,)), ((), ())), preferred_element_type=jnp.float32
    )


def contract_first(left_mat, right_mat):
    return lax.dot_general(
        left_mat, right_mat, (((0,), (0,)), ((), ())), preferred_element_type=jnp.float32
    )


def local(
    tokens,
    seq_lengths,
    cotangent,
    ln1_gain,
    ln1_shift,
    w_qkv,
    b_qkv,
    w_out,
    b_out,
    ln2_gain,
    ln2_shift,
    w_up,
    b_up,
    w_down,
    b_down,
):
    local_rows = tokens.shape[0]
    group_rows = local_rows * lax.axis_size("tensor")
    seq_count = seq_lengths.shape[0]
    qkv_width = w_qkv.shape[2]
    local_heads = qkv_width // HEAD_DIM
    head_scale = HEAD_DIM ** (-0.5)
    block_rows = min(512, SEQ)
    cosine, sine_table = rotary_tables()
    resid = tokens.astype(jnp.float32)
    normed_one, norm_one_back = jax.vjp(
        layer_norm, resid, ln1_gain.astype(jnp.float32), ln1_shift.astype(jnp.float32)
    )
    normed_one_low = normed_one.astype(jnp.bfloat16)
    normed_all = lax.all_gather(normed_one_low, "tensor", axis=0, tiled=True)
    qkv_pre = jnp.einsum(
        "td,dcf->tcf", normed_all, w_qkv, preferred_element_type=jnp.float32
    ) + b_qkv.astype(jnp.float32)

    def split_heads(matrix):
        return matrix.reshape(seq_count, SEQ, local_heads, HEAD_DIM)

    def rotate_pair(query_raw, key_raw):
        return (rotate(query_raw, cosine, sine_table), rotate(key_raw, cosine, sine_table))

    (query_rot, key_rot), rotate_back = jax.vjp(
        rotate_pair, split_heads(qkv_pre[:, 0]), split_heads(qkv_pre[:, 1])
    )
    query_low = query_rot.astype(jnp.bfloat16)
    key_low = key_rot.astype(jnp.bfloat16)
    value_low = split_heads(qkv_pre[:, 2]).astype(jnp.bfloat16)

    def attend_fwd(inputs):
        query_seq, key_seq, value_seq, seq_len = inputs
        key_valid = jnp.arange(SEQ) < seq_len
        out_parts = []
        lse_parts = []
        for offset in range(0, SEQ, block_rows):
            query_blk = query_seq[offset : offset + block_rows]
            scores = (
                jnp.einsum("qhe,khe->hqk", query_blk, key_seq, preferred_element_type=jnp.float32)
                * head_scale
            )
            scores = jnp.where(key_valid[None, None, :], scores, mask_fill)
            row_max = jnp.max(scores, axis=-1, keepdims=True)
            shifted = jnp.exp(scores - row_max)
            row_total = jnp.sum(shifted, axis=-1, keepdims=True)
            weights = (shifted / row_total).astype(jnp.bfloat16)
            out_parts.append(
                jnp.einsum("hqk,khe->qhe", weights, value_seq, preferred_element_type=jnp.float32)
            )
            lse_parts.append((row_max + jnp.log(row_total))[..., 0])
        return (jnp.concatenate(out_parts, axis=0), jnp.concatenate(lse_parts, axis=1))

    attended, log_sums = lax.map(attend_fwd, (query_low, key_low, value_low, seq_lengths))
    attn_vals = attended.reshape(group_rows, qkv_width).astype(jnp.bfloat16)
    mixed = (
        resid
        + lax.psum_scatter(
            jnp.dot(
                lax.slice_in_dim(attn_vals, 0, local_rows * lax.axis_size("tensor"), axis=0),
                w_out,
                preferred_element_type=jnp.float32,
            ),
            "tensor",
            scatter_dimension=0,
            tiled=True,
        )
        + b_out.astype(jnp.float32)
    )
    normed_two, norm_two_back = jax.vjp(
        layer_norm, mixed, ln2_gain.astype(jnp.float32), ln2_shift.astype(jnp.float32)
    )
    normed_two_low = normed_two.astype(jnp.bfloat16)
    grad_out = cotangent.astype(jnp.float32)
    normed_two_all = lax.all_gather(normed_two_low, "tensor", axis=0, tiled=True)
    pre_act = jnp.dot(normed_two_all, w_up, preferred_element_type=jnp.float32) + b_up.astype(
        jnp.float32
    )
    act_vals, gelu_back = jax.vjp(jax.nn.gelu, pre_act)
    act_low = act_vals.astype(jnp.bfloat16)
    ffn_vals = lax.psum_scatter(
        jnp.dot(
            lax.slice_in_dim(act_low, 0, local_rows * lax.axis_size("tensor"), axis=0),
            w_down,
            preferred_element_type=jnp.float32,
        ).astype(jnp.bfloat16),
        "tensor",
        scatter_dimension=0,
        tiled=True,
    ).astype(jnp.float32)
    output = (mixed + ffn_vals + b_down.astype(jnp.float32)).astype(jnp.bfloat16)
    cot_all = lax.all_gather(cotangent, "tensor", axis=0, tiled=True)
    d_act = contract_last(cot_all, w_down)
    grad_w_down = contract_first(act_low, cot_all)
    d_pre = gelu_back(d_act)[0].astype(jnp.bfloat16)
    grad_w_up = contract_first(normed_two_all, d_pre)
    grad_b_up = jnp.sum(d_pre.astype(jnp.float32), axis=0)
    d_normed_two = lax.psum_scatter(
        contract_last(
            lax.slice_in_dim(d_pre, 0, local_rows * lax.axis_size("tensor"), axis=0), w_up
        ),
        "tensor",
        scatter_dimension=0,
        tiled=True,
    )
    d_mixed_norm, grad_gain_two, grad_shift_two = norm_two_back(d_normed_two)
    d_mixed = grad_out + d_mixed_norm
    d_branch = d_mixed.astype(jnp.bfloat16)
    branch_all = lax.all_gather(d_branch, "tensor", axis=0, tiled=True)
    grad_w_out = contract_first(attn_vals, branch_all)
    d_vals = contract_last(branch_all, w_out).astype(jnp.bfloat16)

    def attend_back(inputs):
        query_seq, key_seq, value_seq, dout_seq, lse_seq, seq_len = inputs
        key_valid = jnp.arange(SEQ) < seq_len
        dquery_parts = []
        dkey_sum = jnp.zeros(key_seq.shape, jnp.float32)
        dvalue_sum = jnp.zeros(value_seq.shape, jnp.float32)
        for offset in range(0, SEQ, block_rows):
            query_blk = query_seq[offset : offset + block_rows]
            dout_blk = dout_seq[offset : offset + block_rows]
            lse_blk = lse_seq[:, offset : offset + block_rows]
            scores = (
                jnp.einsum("qhe,khe->hqk", query_blk, key_seq, preferred_element_type=jnp.float32)
                * head_scale
            )
            scores = jnp.where(key_valid[None, None, :], scores, mask_fill)
            probs = jnp.exp(scores - lse_blk[:, :, None])
            weights = probs.astype(jnp.bfloat16)
            dvalue_sum = dvalue_sum + jnp.einsum(
                "hqk,qhe->khe", weights, dout_blk, preferred_element_type=jnp.float32
            )
            d_probs = jnp.einsum(
                "qhe,khe->hqk", dout_blk, value_seq, preferred_element_type=jnp.float32
            )
            inner_sum = jnp.sum(probs * d_probs, axis=-1, keepdims=True)
            d_scores = (probs * (d_probs - inner_sum)).astype(jnp.bfloat16)
            dquery_parts.append(
                jnp.einsum("hqk,khe->qhe", d_scores, key_seq, preferred_element_type=jnp.float32)
                * head_scale
            )
            dkey_sum = (
                dkey_sum
                + jnp.einsum(
                    "hqk,qhe->khe", d_scores, query_blk, preferred_element_type=jnp.float32
                )
                * head_scale
            )
        return (jnp.concatenate(dquery_parts, axis=0), dkey_sum, dvalue_sum)

    d_query, d_key, d_values = lax.map(
        attend_back, (query_low, key_low, value_low, split_heads(d_vals), log_sums, seq_lengths)
    )
    d_query_raw, d_key_raw = rotate_back((d_query, d_key))
    d_qkv = jnp.stack(
        [
            d_query_raw.reshape(group_rows, qkv_width),
            d_key_raw.reshape(group_rows, qkv_width),
            d_values.reshape(group_rows, qkv_width),
        ],
        axis=1,
    ).astype(jnp.bfloat16)
    grad_w_qkv = jnp.einsum("td,tcf->dcf", normed_all, d_qkv, preferred_element_type=jnp.float32)
    grad_b_qkv = jnp.sum(d_qkv.astype(jnp.float32), axis=0)
    d_normed_one = lax.psum_scatter(
        jnp.einsum(
            "tcf,dcf->td",
            lax.slice_in_dim(d_qkv, 0, local_rows * lax.axis_size("tensor"), axis=0),
            w_qkv,
            preferred_element_type=jnp.float32,
        ),
        "tensor",
        scatter_dimension=0,
        tiled=True,
    )
    d_resid_norm, grad_gain_one, grad_shift_one = norm_one_back(d_normed_one)
    grad_tokens = (d_mixed + d_resid_norm).astype(jnp.bfloat16)
    grad_w_qkv, grad_b_qkv, grad_w_out, grad_w_up, grad_b_up, grad_w_down = lax.psum(
        (grad_w_qkv, grad_b_qkv, grad_w_out, grad_w_up, grad_b_up, grad_w_down), "dp"
    )
    shared_local = jnp.stack(
        [
            grad_gain_one,
            grad_shift_one,
            jnp.sum(d_mixed, axis=0),
            grad_gain_two,
            grad_shift_two,
            jnp.sum(grad_out, axis=0),
        ]
    )
    shared_sum = lax.psum(shared_local, ("dp", "tensor"))
    return (
        output,
        grad_tokens,
        shared_sum[0],
        shared_sum[1],
        grad_w_qkv,
        grad_b_qkv,
        grad_w_out,
        shared_sum[2],
        shared_sum[3],
        shared_sum[4],
        grad_w_up,
        grad_b_up,
        grad_w_down,
        shared_sum[5],
    )


def solution(mesh):
    placed = (
        P(("dp", "tensor"), None),
        P("dp"),
        P(("dp", "tensor"), None),
        P(),
        P(),
        P(None, None, "tensor"),
        P(None, "tensor"),
        P("tensor", None),
        P(),
        P(),
        P(),
        P(None, "tensor"),
        P("tensor"),
        P("tensor", None),
        P(),
    )
    return jax.shard_map(
        local,
        mesh=mesh,
        in_specs=placed,
        out_specs=(
            P(("dp", "tensor"), None),
            P(("dp", "tensor"), None),
            P(),
            P(),
            P(None, None, "tensor"),
            P(None, "tensor"),
            P("tensor", None),
            P(),
            P(),
            P(),
            P(None, "tensor"),
            P("tensor"),
            P("tensor", None),
            P(),
        ),
        check_vma=False,
    )
```

profile of v0, /device:TPU:0, one launch (start us, length us, event | category | flops | bytes accessed | tf_op | source)
XLA Modules:
  0.0 759.7 jit_solution(15909219942713301804)
XLA Ops:
  17.8 28.2 %all-gather.5.cloned.1.call-done = bf16[2048,768]{1,0:T(8,128)(2,1)} async-done(((bf16[512,768]{1,0:T(8,128)(2,1)}), bf16[2048,768]{1,0:T(8,128)(2,1)}) %all-gather.5.cloned.1.call-update) | async-done | bytes 3145744 | tf_op jit(solution)/shard_map/all_gather | solution.py:86
  64.9 24.7 %while.28 = (s32[]{:T(128)}, bf16[2,1024,3,64]{1,3,2,0:T(8,128)(2,1)}, f32[2,3,1024]{2,1,0:T(4,128)}, bf16[2,1024,3,64]{1,3,2,0:T(8,128)(2,1)S(1)}, s32[2]{0:T(1...) while((s32[]{:T(128)}, ...), condition=%wide.region_7.8_spmd.clone, body=%wide.region_2.7_spmd.sunk.clone | while | flops 843842560 | bytes 47532784 | solution.py:126
  98.0 57.6 %reduce-scatter.5.cloned.1.call-done = f32[512,768]{1,0:T(8,128)} async-done(((f32[2048,768]{1,0:T(8,128)}), f32[512,768]{1,0:T(8,128)}) %reduce-scatter.5.cloned.1.call-update) | async-done | bytes 1572880 | tf_op jit(solution)/shard_map/reduce_scatter | solution.py:130
  160.4 28.0 %all-gather.7.cloned.1.call-done = bf16[2048,768]{1,0:T(8,128)(2,1)} async-done(((bf16[512,768]{1,0:T(8,128)(2,1)}), bf16[2048,768]{1,0:T(8,128)(2,1)}) %all-gather.7.cloned.1.call-update) | async-done | bytes 3145744 | tf_op jit(solution)/shard_map/all_gather | solution.py:147
  188.4 7.5 fusion.120
  195.9 22.5 %all-gather.9.cloned.1.call-done = bf16[2048,768]{1,0:T(8,128)(2,1)} async-done(((bf16[512,768]{1,0:T(8,128)(2,1)}), bf16[2048,768]{1,0:T(8,128)(2,1)}) %all-gather.9.cloned.1.call-update) | async-done | bytes 3145744 | tf_op jit(solution)/shard_map/all_gather | solution.py:164
  218.3 12.4 %convert_reduce_fusion = (f32[768]{0:T(1024)}, bf16[2048,768]{1,0:T(8,128)(2,1)S(1)}, bf16[2048,768]{1,0:T(8,128)(2,1)}) fusion(f32[2048,768]{1,0:T(8,128)} %fusion.120, f32[768]{0:T(1024)S(1)} %convert_element_type.109, bf16[2048,768]{1,0:T(8,128)(2,1)} %all-gather.9.cloned.1.call-done, bf16[768,768]{1,0:T(8,128)(2,1)S(1)} %copy-done), kind=kOutput, calls=%fused_computation.112 | convolution fusion | flops 2455239936 | bytes 16914432 | tf_op jit(solution)/shard_map/dot_general | solution.py:45
  232.5 4.5 fusion.121
  237.1 6.5 convolution_convert_fusion
  244.3 51.7 %reduce-scatter.9.cloned.1.call-done = f32[512,768]{1,0:T(8,128)} async-done(((f32[2048,768]{1,0:T(8,128)}), f32[512,768]{1,0:T(8,128)}) %reduce-scatter.9.cloned.1.call-update) | async-done | bytes 1572880 | tf_op jit(solution)/shard_map/reduce_scatter | solution.py:170
  299.2 37.2 %reduce-scatter.7.cloned.1.call-done = bf16[512,768]{1,0:T(8,128)(2,1)} async-done(((bf16[2048,768]{1,0:T(8,128)(2,1)}), bf16[512,768]{1,0:T(8,128)(2,1)}) %reduce-scatter.7.cloned.1.call-update) | async-done | bytes 786448 | tf_op jit(solution)/shard_map/reduce_scatter | solution.py:153
  342.6 28.4 %all-gather.11.cloned.1.call-done = bf16[2048,768]{1,0:T(8,128)(2,1)} async-done(((bf16[512,768]{1,0:T(8,128)(2,1)}), bf16[2048,768]{1,0:T(8,128)(2,1)}) %all-gather.11.cloned.1.call-update) | async-done | bytes 3145744 | tf_op jit(solution)/shard_map/all_gather | solution.py:181
  376.9 56.3 %while.29 = (s32[]{:T(128)}, f32[2,1024,3,64]{1,3,2,0:T(8,128)}, f32[2,1024,3,64]{1,3,2,0:T(8,128)}, bf16[2,1024,3,64]{1,3,2,0:T(8,128)(2,1)S(1)}, bf16[2,1024,3...) while((s32[]{:T(128)}, f32[2,1024,3,64]{1,3,2,0:T(8,128)}, ...), condition=%wide.region_18.19_spmd.clone, body=%wide.region_15.18_spmd.sunk.clone | while | flops 2061432832 | bytes 165286976 | solution.py:223
  387.6 4.8 multiply_reduce_fusion.7
  392.5 4.0 multiply_convert_fusion.5
  415.7 4.8 multiply_reduce_fusion.7
  420.5 4.0 multiply_convert_fusion.5
  444.3 4.6 convolution_bitcast_fusion
  449.3 7.1 fusion.124
  456.3 4.2 fusion.123
  469.0 22.1 %all-reduce.4 = (f32[3,192]{1,0:T(4,128)}, f32[768]{0:T(1024)}) all-reduce(f32[3,192]{1,0:T(4,128)S(1)} %convert_reduce_fusion.1, f32[768]{0:T(1024)S(1)} %copy-done.56), channel_id=1, replica_groups=mesh['dp'=8,'tensor'=4] {'dp'}, use_global_device_ids=true, to_apply=%region_31.32 | all-reduce | flops 1344 | bytes 10752 | tf_op jit(solution)/shard_map/psum | solution.py:250
  491.2 16.8 %reduce-scatter.11.cloned.1.call-done = f32[512,768]{1,0:T(8,128)} async-done(((f32[2048,768]{1,0:T(8,128)}), f32[512,768]{1,0:T(8,128)}) %reduce-scatter.11.cloned.1.call-update) | async-done | bytes 1572880 | tf_op jit(solution)/shard_map/reduce_scatter | solution.py:237
  512.6 43.9 %psum.49 = f32[6,768]{1,0:T(8,128)S(1)} all-reduce(f32[6,768]{1,0:T(8,128)S(1)} %stack.20), channel_id=1, replica_groups=mesh['dp'=8,'tensor'=4] {'dp','tensor'}, use_global_device_ids=true, to_apply=%region_28.29 | all-reduce | flops 4608 | bytes 36864 | tf_op jit(solution)/shard_map/psum | solution.py:263
  557.1 189.1 %all-reduce.8.cloned.1.call-done = (f32[768,3,192]{0,2,1:T(8,128)}, f32[192,768]{1,0:T(8,128)}, f32[768,768]{1,0:T(8,128)}, f32[768,768]{1,0:T(8,128)}) async-done(((f32[768,3,192]{0,2,1:T(8,128)}, f32[192,768]{1,0:T(8,128)}, f32[768,768]{1,0:T(8,128)}, f32[768,768]{1,0:T(8,128)}), (f32[768,3,192]{0,2,1:T(8,128)}, f32[192,768]{1,0:T(8,128)}, f32[768,768]{1,0:T(8,128)}, ...) | async-done | bytes 7077904 | tf_op jit(solution)/shard_map/psum | solution.py:250
  (322 shorter events, 153.6 us)
Async XLA Ops:
  7.2 211.2 %copy-start = (bf16[768,768]{1,0:T(8,128)(2,1)S(1)}, bf16[768,768]{1,0:T(8,128)(2,1)}, u32[]{:S(2)}) copy-start(bf16[768,768]{1,0:T(8,128)(2,1)} %param.32) | copy-start | bytes 3538948
  7.2 38.8 %copy-start.65 = (bf16[768,3,192]{0,2,1:T(8,128)(2,1)S(1)}, bf16[768,3,192]{0,2,1:T(8,128)(2,1)}, u32[]{:S(2)}) copy-start(bf16[768,3,192]{0,2,1:T(8,128)(2,1)} %param.24) | copy-start | bytes 2654212
  7.2 38.8 %all-gather.5.cloned.1.call-start = ((), (), s32[]{:S(2)}) async-start(), calls=%async_computation.4 | async-start | bytes 3932160 | tf_op jit(solution)/shard_map/all_gather | solution.py:86
  14.6 141.1 %reduce-scatter.5.cloned.1.call-start = ((), (), s32[]{:S(2)}) async-start(), calls=%async_computation.5 | async-start | bytes 7864320 | tf_op jit(solution)/shard_map/reduce_scatter | solution.py:130
  96.6 59.0 %copy-start.7 = (bf16[512,768]{1,0:T(8,128)(2,1)S(1)}, bf16[512,768]{1,0:T(8,128)(2,1)}, u32[]{:S(2)}) copy-start(bf16[512,768]{1,0:T(8,128)(2,1)} %param.19) | copy-start | bytes 2359300
  96.7 91.7 %all-gather.7.cloned.1.call-start = ((), (), s32[]{:S(2)}) async-start(), calls=%async_computation.6 | async-start | bytes 3932160 | tf_op jit(solution)/shard_map/all_gather | solution.py:147
  159.7 58.6 %all-gather.9.cloned.1.call-start = ((), (), s32[]{:S(2)}) async-start(), calls=%async_computation.8 | async-start | bytes 3932160 | tf_op jit(solution)/shard_map/all_gather | solution.py:164
  160.3 135.8 %reduce-scatter.9.cloned.1.call-start = ((), (), s32[]{:S(2)}) async-start(), calls=%async_computation.9 | async-start | bytes 7864320 | tf_op jit(solution)/shard_map/reduce_scatter | solution.py:170
  237.1 99.3 %reduce-scatter.7.cloned.1.call-start = ((), (), s32[]{:S(2)}) async-start(), calls=%async_computation.7 | async-start | bytes 3932160 | tf_op jit(solution)/shard_map/reduce_scatter | solution.py:153
  243.7 127.3 %all-gather.11.cloned.1.call-start = ((), (), s32[]{:S(2)}) async-start(), calls=%async_computation.10 | async-start | bytes 3932160 | tf_op jit(solution)/shard_map/all_gather | solution.py:181
  299.1 42.0 %copy-start.22 = (bf16[512,768]{1,0:T(8,128)(2,1)S(1)}, bf16[512,768]{1,0:T(8,128)(2,1)}, u32[]{:S(2)}) copy-start(bf16[512,768]{1,0:T(8,128)(2,1)} %param.21) | copy-start | bytes 2359300
  340.0 31.0 %copy-start.40 = (bf16[192,768]{1,0:T(8,128)(2,1)S(1)}, bf16[192,768]{1,0:T(8,128)(2,1)}, u32[]{:S(2)}) copy-start(bf16[192,768]{1,0:T(8,128)(2,1)} %param.26) | copy-start | bytes 884740
  340.0 34.0 %copy-start.52 = (f32[512]{0:T(512)}, f32[512]{0:T(512)S(1)}, u32[]{:S(2)}) copy-start(f32[512]{0:T(512)S(1)} %negate_multiply_fusion.1) | copy-start | bytes 6148
  342.3 165.6 %reduce-scatter.11.cloned.1.call-start = ((), (), s32[]{:S(2)}) async-start(), calls=%async_computation.11 | async-start | bytes 7864320 | tf_op jit(solution)/shard_map/reduce_scatter | solution.py:237
  444.3 17.9 %copy-start.24 = (bf16[2048,3,192]{0,2,1:T(8,128)(2,1)}, bf16[2048,3,192]{0,2,1:T(8,128)(2,1)S(1)}, u32[]{:S(2)}) copy-start(bf16[2048,3,192]{0,2,1:T(8,128)(2,1)S(1)} %constant_dynamic-update-slice_fusion) | copy-start | bytes 7077892
  448.9 297.3 %all-reduce.8.cloned.1.call-start = ((), (), s32[]{:S(2)}) async-start(), calls=%async_computation.12 | async-start | bytes 14155776 | tf_op jit(solution)/shard_map/psum | solution.py:250
  466.1 41.9 %copy-start.8 = (bf16[512,768]{1,0:T(8,128)(2,1)S(1)}, bf16[512,768]{1,0:T(8,128)(2,1)}, u32[]{:S(2)}) copy-start(bf16[512,768]{1,0:T(8,128)(2,1)} %param.19) | copy-start | bytes 2359300
  466.1 41.9 %copy-start.45 = (f32[768]{0:T(1024)S(1)}, f32[768]{0:T(1024)}, u32[]{:S(2)}) copy-start(f32[768]{0:T(1024)} %copy-done.44) | copy-start | bytes 9220
  466.1 41.8 %copy-start.47 = (f32[512]{0:T(512)S(1)}, f32[512]{0:T(512)}, u32[]{:S(2)}) copy-start(f32[512]{0:T(512)} %copy-done.46) | copy-start | bytes 6148
  466.1 43.8 %copy-start.51 = (f32[512]{0:T(512)S(1)}, f32[512]{0:T(512)}, u32[]{:S(2)}) copy-start(f32[512]{0:T(512)} %copy-done.50) | copy-start | bytes 6148
  466.2 43.8 %copy-start.49 = (f32[512]{0:T(512)S(1)}, f32[512]{0:T(512)}, u32[]{:S(2)}) copy-start(f32[512]{0:T(512)} %copy-done.48) | copy-start | bytes 6148
  466.8 44.0 %copy-start.13 = (f32[512,768]{1,0:T(8,128)S(1)}, f32[512,768]{1,0:T(8,128)}, u32[]{:S(2)}) copy-start(f32[512,768]{1,0:T(8,128)} %copy-done.12) | copy-start | bytes 4718596
  466.8 44.0 %copy-start.23 = (bf16[512,768]{1,0:T(8,128)(2,1)S(1)}, bf16[512,768]{1,0:T(8,128)(2,1)}, u32[]{:S(2)}) copy-start(bf16[512,768]{1,0:T(8,128)(2,1)} %param.21) | copy-start | bytes 2359300
  466.8 44.0 %copy-start.53 = (f32[512]{0:T(512)S(1)}, f32[512]{0:T(512)}, u32[]{:S(2)}) copy-start(f32[512]{0:T(512)} %copy-done.52) | copy-start | bytes 6148
  (73 other events, 213.0 us)
Sparse Core Ops, SparseCore 0:
  14.7 31.2 all-gather.4
  96.8 58.8 reduce-scatter.4
  159.8 28.4 all-gather.6
  189.8 28.4 all-gather.8
  237.2 58.8 reduce-scatter.8
  298.4 37.8 reduce-scatter.6
  342.5 28.4 all-gather.10
  449.1 58.8 reduce-scatter.10
  513.5 232.7 all-reduce.7
where the time goes:
time: 764 us; the launch traced here: 760 us
  waiting for transfers between devices  460 us (60%)
  matrix products  111 us (15%)
  blocking collectives  66 us (9%)
  local copies, waits for them, and re-layouts  61.2 us (8%)
  other arithmetic  44.7 us (6%)
  between operations  14.8 us (2%)
    psum x1, waiting for transfers between devices, local(): lax.psum((grad_w_qkv, grad_b_qkv, grad_w_out, grad_w_up, grad_b_up, grad_...  189 us
    reduce_scatter x1, waiting for transfers between devices, local(): lax.psum_scatter(jnp.dot(lax.slice_in_dim(attn_vals, 0, local_rows * lax....  57.6 us
    reduce_scatter x1, waiting for transfers between devices, local(): lax.psum_scatter(contract_last(lax.slice_in_dim(d_pre, 0, local_rows * la...  51.7 us
    psum x1, blocking collectives, local(): shared_sum = lax.psum(shared_local, ('dp', 'tensor'))  43.9 us
    reduce_scatter x1, waiting for transfers between devices, local(): lax.psum_scatter(jnp.dot(lax.slice_in_dim(act_low, 0, local_rows * lax.ax...  37.2 us
    all_gather x1, waiting for transfers between devices, local(): branch_all = lax.all_gather(d_branch, 'tensor', axis=0, tiled=True)  28.4 us
    all_gather x1, waiting for transfers between devices, local(): normed_all = lax.all_gather(normed_one_low, 'tensor', axis=0, tiled=True)  28.2 us
    all_gather x1, waiting for transfers between devices, local(): lax.all_gather(normed_two_low, 'tensor', axis=0, tiled=True)  28 us
  transfers between devices with their start and end apart: 9, of which 9 were waited for; matrix products, arithmetic and copies ran while one was open for 6% of the time, Pallas kernels for 0%

commit v1 on v0

--- a/solution.py
+++ b/solution.py
@@ -260,7 +260,7 @@
             jnp.sum(grad_out, axis=0),
         ]
     )
-    shared_sum = lax.psum(shared_local, ("dp", "tensor"))
+    shared_sum = jnp.sum(lax.all_gather(shared_local, ("dp", "tensor")), axis=0)
     return (
         output,
         grad_tokens,

time: 764 us -> 767 us (level)
    all_gather x0 -> x1, blocking collectives: none -> 48 us  [local(): shared_sum = jnp.sum(lax.all_gather(shared_local, ('dp', 'tensor')), axis=0)]
    psum x1 -> x0, blocking collectives: 43.9 us -> none  [local(): shared_sum = lax.psum(shared_local, ('dp', 'tensor'))]
where the time goes in v1:
time: 767 us; the launch traced here: 763 us
  waiting for transfers between devices  459 us (60%)
  matrix products  111 us (14%)
  blocking collectives  70.2 us (9%)
  local copies, waits for them, and re-layouts  61.2 us (8%)
  other arithmetic  44.7 us (6%)
  between operations  14.8 us (2%)
    psum x1, waiting for transfers between devices, local(): lax.psum((grad_w_qkv, grad_b_qkv, grad_w_out, grad_w_up, grad_b_up, grad_...  188 us
    reduce_scatter x1, waiting for transfers between devices, local(): lax.psum_scatter(jnp.dot(lax.slice_in_dim(attn_vals, 0, local_rows * lax....  57.6 us
    reduce_scatter x1, waiting for transfers between devices, local(): lax.psum_scatter(contract_last(lax.slice_in_dim(d_pre, 0, local_rows * la...  51.7 us
    all_gather x1, blocking collectives, local(): shared_sum = jnp.sum(lax.all_gather(shared_local, ('dp', 'tensor')), axis=0)  48 us
    reduce_scatter x1, waiting for transfers between devices, local(): lax.psum_scatter(jnp.dot(lax.slice_in_dim(act_low, 0, local_rows * lax.ax...  37.2 us
    all_gather x1, waiting for transfers between devices, local(): branch_all = lax.all_gather(d_branch, 'tensor', axis=0, tiled=True)  28.4 us
    all_gather x1, waiting for transfers between devices, local(): normed_all = lax.all_gather(normed_one_low, 'tensor', axis=0, tiled=True)  28.2 us
    all_gather x1, waiting for transfers between devices, local(): lax.all_gather(normed_two_low, 'tensor', axis=0, tiled=True)  28 us
  transfers between devices with their start and end apart: 9, of which 9 were waited for; matrix products, arithmetic and copies ran while one was open for 6% of the time, Pallas kernels for 0%

profile of v1, /device:TPU:0, one launch (start us, length us, event | category | flops | bytes accessed | tf_op | source)
XLA Modules:
  0.0 762.5 jit_solution(14221184813300642260)
XLA Ops:
  17.8 28.2 %all-gather.7.cloned.1.call-done = bf16[2048,768]{1,0:T(8,128)(2,1)} async-done(((bf16[512,768]{1,0:T(8,128)(2,1)}), bf16[2048,768]{1,0:T(8,128)(2,1)}) %all-gather.7.cloned.1.call-update) | async-done | bytes 3145744 | tf_op jit(solution)/shard_map/all_gather | solution.py:86
  64.9 24.7 %while.28 = (s32[]{:T(128)}, bf16[2,1024,3,64]{1,3,2,0:T(8,128)(2,1)}, f32[2,3,1024]{2,1,0:T(4,128)}, bf16[2,1024,3,64]{1,3,2,0:T(8,128)(2,1)S(1)}, s32[2]{0:T(1...) while((s32[]{:T(128)}, ...), condition=%wide.region_7.8_spmd.clone, body=%wide.region_2.7_spmd.sunk.clone | while | flops 843842560 | bytes 47532784 | solution.py:126
  98.0 57.6 %reduce-scatter.5.cloned.1.call-done = f32[512,768]{1,0:T(8,128)} async-done(((f32[2048,768]{1,0:T(8,128)}), f32[512,768]{1,0:T(8,128)}) %reduce-scatter.5.cloned.1.call-update) | async-done | bytes 1572880 | tf_op jit(solution)/shard_map/reduce_scatter | solution.py:130
  160.4 28.0 %all-gather.9.cloned.1.call-done = bf16[2048,768]{1,0:T(8,128)(2,1)} async-done(((bf16[512,768]{1,0:T(8,128)(2,1)}), bf16[2048,768]{1,0:T(8,128)(2,1)}) %all-gather.9.cloned.1.call-update) | async-done | bytes 3145744 | tf_op jit(solution)/shard_map/all_gather | solution.py:147
  188.4 7.5 fusion.120
  195.9 22.5 %all-gather.11.cloned.1.call-done = bf16[2048,768]{1,0:T(8,128)(2,1)} async-done(((bf16[512,768]{1,0:T(8,128)(2,1)}), bf16[2048,768]{1,0:T(8,128)(2,1)}) %all-gather.11.cloned.1.call-update) | async-done | bytes 3145744 | tf_op jit(solution)/shard_map/all_gather | solution.py:164
  218.3 12.4 %convert_reduce_fusion = (f32[768]{0:T(1024)}, bf16[2048,768]{1,0:T(8,128)(2,1)S(1)}, bf16[2048,768]{1,0:T(8,128)(2,1)}) fusion(f32[2048,768]{1,0:T(8,128)} %fusion.120, f32[768]{0:T(1024)S(1)} %convert_element_type.109, bf16[2048,768]{1,0:T(8,128)(2,1)} %all-gather.11.cloned.1.call-done, bf16[768,768]{1,0:T(8,128)(2,1)S(1)} %copy-done), kind=kOutput, calls=%fused_computation.112 | convolution fusion | flops 2455239936 | bytes 16914432 | tf_op jit(solution)/shard_map/dot_general | solution.py:45
  232.5 4.5 fusion.121
  237.1 6.5 convolution_convert_fusion
  244.3 51.7 %reduce-scatter.9.cloned.1.call-done = f32[512,768]{1,0:T(8,128)} async-done(((f32[2048,768]{1,0:T(8,128)}), f32[512,768]{1,0:T(8,128)}) %reduce-scatter.9.cloned.1.call-update) | async-done | bytes 1572880 | tf_op jit(solution)/shard_map/reduce_scatter | solution.py:170
  299.2 37.2 %reduce-scatter.7.cloned.1.call-done = bf16[512,768]{1,0:T(8,128)(2,1)} async-done(((bf16[2048,768]{1,0:T(8,128)(2,1)}), bf16[512,768]{1,0:T(8,128)(2,1)}) %reduce-scatter.7.cloned.1.call-update) | async-done | bytes 786448 | tf_op jit(solution)/shard_map/reduce_scatter | solution.py:153
  342.6 28.4 %all-gather.13.cloned.1.call-done = bf16[2048,768]{1,0:T(8,128)(2,1)} async-done(((bf16[512,768]{1,0:T(8,128)(2,1)}), bf16[2048,768]{1,0:T(8,128)(2,1)}) %all-gather.13.cloned.1.call-update) | async-done | bytes 3145744 | tf_op jit(solution)/shard_map/all_gather | solution.py:181
  376.9 56.3 %while.29 = (s32[]{:T(128)}, f32[2,1024,3,64]{1,3,2,0:T(8,128)}, f32[2,1024,3,64]{1,3,2,0:T(8,128)}, bf16[2,1024,3,64]{1,3,2,0:T(8,128)(2,1)S(1)}, bf16[2,1024,3...) while((s32[]{:T(128)}, f32[2,1024,3,64]{1,3,2,0:T(8,128)}, ...), condition=%wide.region_18.19_spmd.clone, body=%wide.region_15.18_spmd.sunk.clone | while | flops 2061432832 | bytes 165286976 | solution.py:223
  387.6 4.8 multiply_reduce_fusion.7
  392.5 4.0 multiply_convert_fusion.5
  415.7 4.8 multiply_reduce_fusion.7
  420.5 4.0 multiply_convert_fusion.5
  444.3 4.6 convolution_bitcast_fusion
  449.3 7.1 fusion.124
  456.3 4.2 fusion.123
  469.0 22.1 %all-reduce.4 = (f32[3,192]{1,0:T(4,128)}, f32[768]{0:T(1024)}) all-reduce(f32[3,192]{1,0:T(4,128)S(1)} %convert_reduce_fusion.1, f32[768]{0:T(1024)S(1)} %copy-done.56), channel_id=1, replica_groups=mesh['dp'=8,'tensor'=4] {'dp'}, use_global_device_ids=true, to_apply=%region_31.32 | all-reduce | flops 1344 | bytes 10752 | tf_op jit(solution)/shard_map/psum | solution.py:250
  491.2 16.8 %reduce-scatter.11.cloned.1.call-done = f32[512,768]{1,0:T(8,128)} async-done(((f32[2048,768]{1,0:T(8,128)}), f32[512,768]{1,0:T(8,128)}) %reduce-scatter.11.cloned.1.call-update) | async-done | bytes 1572880 | tf_op jit(solution)/shard_map/reduce_scatter | solution.py:237
  512.6 48.0 %all-gather.1 = f32[32,6,768]{2,1,0:T(8,128)S(1)} all-gather(f32[1,6,768]{2,1,0:T(8,128)S(1)} %bitcast.262), channel_id=2, replica_groups=mesh['dp'=8,'tensor'=4] {'dp','tensor'}, dimensions={0}, use_global_device_ids=true | all-gather | bytes 608256 | tf_op jit(solution)/shard_map/all_gather | solution.py:263
  561.4 187.7 %all-reduce.8.cloned.1.call-done = (f32[768,3,192]{0,2,1:T(8,128)}, f32[192,768]{1,0:T(8,128)}, f32[768,768]{1,0:T(8,128)}, f32[768,768]{1,0:T(8,128)}) async-done(((f32[768,3,192]{0,2,1:T(8,128)}, f32[192,768]{1,0:T(8,128)}, f32[768,768]{1,0:T(8,128)}, f32[768,768]{1,0:T(8,128)}), (f32[768,3,192]{0,2,1:T(8,128)}, f32[192,768]{1,0:T(8,128)}, f32[768,768]{1,0:T(8,128)}, ...) | async-done | bytes 7077904 | tf_op jit(solution)/shard_map/psum | solution.py:250
  (323 shorter events, 153.7 us)
Async XLA Ops:
  7.2 211.2 %copy-start = (bf16[768,768]{1,0:T(8,128)(2,1)S(1)}, bf16[768,768]{1,0:T(8,128)(2,1)}, u32[]{:S(2)}) copy-start(bf16[768,768]{1,0:T(8,128)(2,1)} %param.32) | copy-start | bytes 3538948
  7.2 38.8 %copy-start.65 = (bf16[768,3,192]{0,2,1:T(8,128)(2,1)S(1)}, bf16[768,3,192]{0,2,1:T(8,128)(2,1)}, u32[]{:S(2)}) copy-start(bf16[768,3,192]{0,2,1:T(8,128)(2,1)} %param.24) | copy-start | bytes 2654212
  7.2 38.8 %all-gather.7.cloned.1.call-start = ((), (), s32[]{:S(2)}) async-start(), calls=%async_computation.4 | async-start | bytes 3932160 | tf_op jit(solution)/shard_map/all_gather | solution.py:86
  14.6 141.1 %reduce-scatter.5.cloned.1.call-start = ((), (), s32[]{:S(2)}) async-start(), calls=%async_computation.5 | async-start | bytes 7864320 | tf_op jit(solution)/shard_map/reduce_scatter | solution.py:130
  96.6 59.0 %copy-start.7 = (bf16[512,768]{1,0:T(8,128)(2,1)S(1)}, bf16[512,768]{1,0:T(8,128)(2,1)}, u32[]{:S(2)}) copy-start(bf16[512,768]{1,0:T(8,128)(2,1)} %param.19) | copy-start | bytes 2359300
  96.7 91.7 %all-gather.9.cloned.1.call-start = ((), (), s32[]{:S(2)}) async-start(), calls=%async_computation.6 | async-start | bytes 3932160 | tf_op jit(solution)/shard_map/all_gather | solution.py:147
  159.7 58.6 %all-gather.11.cloned.1.call-start = ((), (), s32[]{:S(2)}) async-start(), calls=%async_computation.8 | async-start | bytes 3932160 | tf_op jit(solution)/shard_map/all_gather | solution.py:164
  160.3 135.8 %reduce-scatter.9.cloned.1.call-start = ((), (), s32[]{:S(2)}) async-start(), calls=%async_computation.9 | async-start | bytes 7864320 | tf_op jit(solution)/shard_map/reduce_scatter | solution.py:170
  237.1 99.3 %reduce-scatter.7.cloned.1.call-start = ((), (), s32[]{:S(2)}) async-start(), calls=%async_computation.7 | async-start | bytes 3932160 | tf_op jit(solution)/shard_map/reduce_scatter | solution.py:153
  243.7 127.3 %all-gather.13.cloned.1.call-start = ((), (), s32[]{:S(2)}) async-start(), calls=%async_computation.10 | async-start | bytes 3932160 | tf_op jit(solution)/shard_map/all_gather | solution.py:181
  299.1 42.0 %copy-start.22 = (bf16[512,768]{1,0:T(8,128)(2,1)S(1)}, bf16[512,768]{1,0:T(8,128)(2,1)}, u32[]{:S(2)}) copy-start(bf16[512,768]{1,0:T(8,128)(2,1)} %param.21) | copy-start | bytes 2359300
  340.0 31.0 %copy-start.40 = (bf16[192,768]{1,0:T(8,128)(2,1)S(1)}, bf16[192,768]{1,0:T(8,128)(2,1)}, u32[]{:S(2)}) copy-start(bf16[192,768]{1,0:T(8,128)(2,1)} %param.26) | copy-start | bytes 884740
  340.0 34.0 %copy-start.52 = (f32[512]{0:T(512)}, f32[512]{0:T(512)S(1)}, u32[]{:S(2)}) copy-start(f32[512]{0:T(512)S(1)} %negate_multiply_fusion.1) | copy-start | bytes 6148
  342.3 165.6 %reduce-scatter.11.cloned.1.call-start = ((), (), s32[]{:S(2)}) async-start(), calls=%async_computation.11 | async-start | bytes 7864320 | tf_op jit(solution)/shard_map/reduce_scatter | solution.py:237
  444.3 17.9 %copy-start.24 = (bf16[2048,3,192]{0,2,1:T(8,128)(2,1)}, bf16[2048,3,192]{0,2,1:T(8,128)(2,1)S(1)}, u32[]{:S(2)}) copy-start(bf16[2048,3,192]{0,2,1:T(8,128)(2,1)S(1)} %constant_dynamic-update-slice_fusion) | copy-start | bytes 7077892
  448.9 300.2 %all-reduce.8.cloned.1.call-start = ((), (), s32[]{:S(2)}) async-start(), calls=%async_computation.12 | async-start | bytes 14155776 | tf_op jit(solution)/shard_map/psum | solution.py:250
  466.1 41.9 %copy-start.8 = (bf16[512,768]{1,0:T(8,128)(2,1)S(1)}, bf16[512,768]{1,0:T(8,128)(2,1)}, u32[]{:S(2)}) copy-start(bf16[512,768]{1,0:T(8,128)(2,1)} %param.19) | copy-start | bytes 2359300
  466.1 41.9 %copy-start.45 = (f32[768]{0:T(1024)S(1)}, f32[768]{0:T(1024)}, u32[]{:S(2)}) copy-start(f32[768]{0:T(1024)} %copy-done.44) | copy-start | bytes 9220
  466.1 41.8 %copy-start.47 = (f32[512]{0:T(512)S(1)}, f32[512]{0:T(512)}, u32[]{:S(2)}) copy-start(f32[512]{0:T(512)} %copy-done.46) | copy-start | bytes 6148
  466.1 43.8 %copy-start.51 = (f32[512]{0:T(512)S(1)}, f32[512]{0:T(512)}, u32[]{:S(2)}) copy-start(f32[512]{0:T(512)} %copy-done.50) | copy-start | bytes 6148
  466.2 43.8 %copy-start.49 = (f32[512]{0:T(512)S(1)}, f32[512]{0:T(512)}, u32[]{:S(2)}) copy-start(f32[512]{0:T(512)} %copy-done.48) | copy-start | bytes 6148
  466.8 44.0 %copy-start.13 = (f32[512,768]{1,0:T(8,128)S(1)}, f32[512,768]{1,0:T(8,128)}, u32[]{:S(2)}) copy-start(f32[512,768]{1,0:T(8,128)} %copy-done.12) | copy-start | bytes 4718596
  466.8 44.0 %copy-start.23 = (bf16[512,768]{1,0:T(8,128)(2,1)S(1)}, bf16[512,768]{1,0:T(8,128)(2,1)}, u32[]{:S(2)}) copy-start(bf16[512,768]{1,0:T(8,128)(2,1)} %param.21) | copy-start | bytes 2359300
  466.8 44.0 %copy-start.53 = (f32[512]{0:T(512)S(1)}, f32[512]{0:T(512)}, u32[]{:S(2)}) copy-start(f32[512]{0:T(512)} %copy-done.52) | copy-start | bytes 6148
  (73 other events, 213.0 us)
Sparse Core Ops, SparseCore 0:
  14.7 31.2 all-gather.6
  96.8 58.8 reduce-scatter.4
  159.8 28.4 all-gather.8
  189.8 28.4 all-gather.10
  237.2 58.8 reduce-scatter.8
  298.4 37.8 reduce-scatter.6
  342.5 28.4 all-gather.12
  449.1 58.8 reduce-scatter.10
  513.5 235.5 all-reduce.7
